TPU v7x, 32 devices: a whole 2x2x4 slice. The times are simulated.
32 devices in a mesh: dp: 8 (over y, x, core), tensor: 4 (over z).
Axes of the slice: x: 2, y: 2, z: 4, core: 2. Of those that a mesh axis runs over, the one named last changes fastest.
Arguments:
- block_in: bfloat16 [12288, 1536], P(('dp', 'tensor')), may hold values from -6 to 6
- cotangent: bfloat16 [12288, 1536], P(('dp', 'tensor')), may hold values from -6 to 6
- segment_ids: int32 [24, 512], P('dp'), may hold values from 0 to 3, never falling along the last dimension, each value on 1 to 256 neighbouring positions
- attn_gain: bfloat16 [1536], P('dp'), may hold values from 0.5 to 1.5
- qkv_weight: bfloat16 [1536, 3072], P('dp', 'tensor'), may hold values from -4 to 4
- out_weight: bfloat16 [1536, 1536], P('tensor', 'dp'), may hold values from -1.25 to 1.25
- mlp_gain: bfloat16 [1536], P('dp'), may hold values from 0.5 to 1.5
- gate_weight: bfloat16 [1536, 4096], P('dp', 'tensor'), may hold values from -0.15625 to 0.15625
- up_weight: bfloat16 [1536, 4096], P('dp', 'tensor'), may hold values from -0.15625 to 0.15625
- down_weight: bfloat16 [4096, 1536], P('tensor', 'dp'), may hold values from -0.09375 to 0.09375
Outputs:
- block_out: bfloat16 [12288, 1536], P(('dp', 'tensor'))
- input_grad: bfloat16 [12288, 1536], P(('dp', 'tensor'))
- attn_gain_grad: float32 [1536], P('dp')
- qkv_grad: float32 [1536, 3072], P('dp', 'tensor')
- out_grad: float32 [1536, 1536], P('tensor', 'dp')
- mlp_gain_grad: float32 [1536], P('dp')
- gate_grad: float32 [1536, 4096], P('dp', 'tensor')
- up_grad: float32 [1536, 4096], P('dp', 'tensor')
- down_grad: float32 [4096, 1536], P('tensor', 'dp')
Inputs may be any that keep to these rules, and one draw needn't show every extreme that they name: `segment_ids`: segment numbers never fall along a sequence; a segment holds at most 256 tokens of its sequence, and some segment of every sequence holds exactly that many.
All inputs are finite; a program needn't handle non-finite values.
Results may differ from a plain program's by a relative error of at most 0.025.
The roundings to bfloat16 on the way count: a program that leaves them out, or rounds other values in their place, can miss the bound.
Values may be sent and summed in bfloat16 or wider, within the bound.
A program may use at most 192 MiB of HBM per device.

v0:
```python
import jax
import jax.numpy as jnp
from jax import lax
from jax.sharding import PartitionSpec as P

QUERY_HEADS = 16
KEY_VALUE_HEADS = 8
HEAD_SIZE = 96
EPS = 1e-05
ROPE_BASE = 100000.0
NEG_FILL = -1e30


def doc_positions(segments):
    length = segments.shape[1]
    position_index = jnp.broadcast_to(jnp.arange(length, dtype=jnp.int32)[None, :], segments.shape)
    change = jnp.concatenate(
        [jnp.ones((segments.shape[0], 1), dtype=bool), segments[:, 1:] != segments[:, :-1]], axis=1
    )
    starts = lax.cummax(jnp.where(change, position_index, jnp.zeros_like(position_index)), axis=1)
    return position_index - starts


def rotary_tables(segments):
    half_dim = HEAD_SIZE // 2
    frequency = jnp.power(ROPE_BASE, -(2.0 * jnp.arange(half_dim, dtype=jnp.float32)) / HEAD_SIZE)
    angles = doc_positions(segments).astype(jnp.float32)[..., None] * frequency
    cosine_table = jnp.concatenate([jnp.cos(angles), jnp.cos(angles)], axis=-1)
    sine_table = jnp.concatenate([jnp.sin(angles), jnp.sin(angles)], axis=-1)
    return (cosine_table, sine_table)


def rotate(vector, cosine_table, sine_table):
    half_dim = vector.shape[-1] // 2
    turned = jnp.concatenate([-vector[..., half_dim:], vector[..., :half_dim]], axis=-1)
    return vector * cosine_table + turned * sine_table


def unrotate(vector, cosine_table, sine_table):
    half_dim = vector.shape[-1] // 2
    shifted = vector * sine_table
    returned = jnp.concatenate([shifted[..., half_dim:], -shifted[..., :half_dim]], axis=-1)
    return vector * cosine_table + returned


def allowed_pairs(segments):
    length = segments.shape[1]
    offsets = jnp.arange(length)
    causal = offsets[None, :] <= offsets[:, None]
    same_doc = segments[:, :, None] == segments[:, None, :]
    return (causal[None] & same_doc)[:, None, None]


def score_block(queries, key_heads, segments):
    scores = jnp.einsum(
        "sqgrd,skgd->sgrqk", queries, key_heads, preferred_element_type=jnp.float32
    ) * HEAD_SIZE ** (-0.5)
    return jnp.where(allowed_pairs(segments), scores, NEG_FILL)


def rms_scale(features):
    return lax.rsqrt(jnp.mean(features * features, axis=-1, keepdims=True) + EPS)


def norm_back(features, inverse, gain_vector, upstream):
    scaled = gain_vector * upstream
    return inverse * scaled - features * (inverse * inverse * inverse) * jnp.mean(
        scaled * features, axis=-1, keepdims=True
    )


def widen(shard_rows):
    return lax.all_gather(shard_rows, "tensor", axis=0, tiled=True)


def narrow(partial_value):
    return lax.psum_scatter(
        partial_value.astype(jnp.bfloat16), "tensor", scatter_dimension=0, tiled=True
    ).astype(jnp.float32)


def local(
    block_in,
    cotangent,
    segment_ids,
    attn_gain,
    qkv_weight,
    out_weight,
    mlp_gain,
    gate_weight,
    up_weight,
    down_weight,
):
    qkv_full, gate_full, up_full, gain_attn_raw, gain_mlp_raw = (
        lax.all_gather(qkv_weight, "dp", axis=0, tiled=True),
        lax.all_gather(gate_weight, "dp", axis=0, tiled=True),
        lax.all_gather(up_weight, "dp", axis=0, tiled=True),
        lax.all_gather(attn_gain, "dp", axis=0, tiled=True),
        lax.all_gather(mlp_gain, "dp", axis=0, tiled=True),
    )
    out_cols, down_cols = (
        lax.all_gather(out_weight, "dp", axis=1, tiled=True),
        lax.all_gather(down_weight, "dp", axis=1, tiled=True),
    )
    seq_count, length = segment_ids.shape
    repeat_factor = QUERY_HEADS // KEY_VALUE_HEADS
    groups = qkv_full.shape[1] // ((repeat_factor + 2) * HEAD_SIZE)
    gain_attn = gain_attn_raw.astype(jnp.float32)
    gain_mlp = gain_mlp_raw.astype(jnp.float32)
    residual = block_in.astype(jnp.float32)
    scale_attn = rms_scale(residual)
    normed1 = widen((residual * scale_attn * gain_attn).astype(jnp.bfloat16))
    projected = jnp.dot(normed1, qkv_full, preferred_element_type=jnp.float32).reshape(
        seq_count, length, groups, repeat_factor + 2, HEAD_SIZE
    )
    cosine_table, sine_table = rotary_tables(segment_ids)
    cos_query = cosine_table[:, :, None, None, :]
    sin_query = sine_table[:, :, None, None, :]
    cos_key = cosine_table[:, :, None, :]
    sin_key = sine_table[:, :, None, :]
    queries = rotate(projected[:, :, :, :repeat_factor], cos_query, sin_query).astype(jnp.bfloat16)
    key_heads = rotate(projected[:, :, :, repeat_factor], cos_key, sin_key).astype(jnp.bfloat16)
    values = projected[:, :, :, repeat_factor + 1].astype(jnp.bfloat16)
    scores = score_block(queries, key_heads, segment_ids)
    highest = jnp.max(scores, axis=-1, keepdims=True)
    log_total = highest + jnp.log(jnp.sum(jnp.exp(scores - highest), axis=-1, keepdims=True))
    probability = jnp.exp(scores - log_total).astype(jnp.bfloat16)
    attended = jnp.einsum(
        "sgrqk,skgd->sqgrd", probability, values, preferred_element_type=jnp.float32
    ).astype(jnp.bfloat16)
    attn_flat = attended.reshape(seq_count * length, groups * repeat_factor * HEAD_SIZE)
    attn_delta = lax.psum_scatter(
        jnp.dot(attn_flat, out_cols, preferred_element_type=jnp.float32).astype(jnp.bfloat16),
        "tensor",
        scatter_dimension=0,
        tiled=True,
    ).astype(jnp.float32)
    hidden1 = residual + attn_delta
    scale_mlp = rms_scale(hidden1)
    normed2 = widen((hidden1 * scale_mlp * gain_mlp).astype(jnp.bfloat16))
    gate = jnp.dot(normed2, gate_full, preferred_element_type=jnp.float32)
    up_value = jnp.dot(normed2, up_full, preferred_element_type=jnp.float32)
    sigmoid_gate = jax.nn.sigmoid(gate)
    activated = (gate * sigmoid_gate * up_value).astype(jnp.bfloat16)
    mlp_delta = narrow(jnp.dot(activated, down_cols, preferred_element_type=jnp.float32))
    block_out = (hidden1 + mlp_delta).astype(jnp.bfloat16)
    grad_rows = widen(cotangent)
    down_part = jnp.einsum("tf,td->fd", activated, grad_rows, preferred_element_type=jnp.float32)
    act_grad = jnp.einsum("td,fd->tf", grad_rows, down_cols, preferred_element_type=jnp.float32)
    gate_delta = (act_grad * up_value * sigmoid_gate * (1.0 + gate * (1.0 - sigmoid_gate))).astype(
        jnp.bfloat16
    )
    up_delta = (act_grad * gate * sigmoid_gate).astype(jnp.bfloat16)
    gate_part = jnp.einsum("td,tf->df", normed2, gate_delta, preferred_element_type=jnp.float32)
    up_part = jnp.einsum("td,tf->df", normed2, up_delta, preferred_element_type=jnp.float32)
    normed2_term = jnp.einsum(
        "tf,df->td", gate_delta, gate_full, preferred_element_type=jnp.float32
    ) + jnp.einsum("tf,df->td", up_delta, up_full, preferred_element_type=jnp.float32)
    normed2_grad = narrow(normed2_term)
    mlp_gain_part = jnp.sum(normed2_grad * hidden1 * scale_mlp, axis=0)
    hidden1_grad = cotangent.astype(jnp.float32) + norm_back(
        hidden1, scale_mlp, gain_mlp, normed2_grad
    )
    hidden1_rounded = hidden1_grad.astype(jnp.bfloat16)
    grad_full = lax.all_gather(hidden1_rounded, "tensor", axis=0, tiled=True)
    attended_grad = jnp.einsum(
        "td,hd->th", grad_full, out_cols, preferred_element_type=jnp.float32
    ).astype(jnp.bfloat16)
    out_part = jnp.einsum("th,td->hd", attn_flat, grad_full, preferred_element_type=jnp.float32)
    attended_grad = attended_grad.reshape(seq_count, length, groups, repeat_factor, HEAD_SIZE)
    prob_full = jnp.exp(score_block(queries, key_heads, segment_ids) - log_total)
    prob_grad = jnp.einsum(
        "sqgrd,skgd->sgrqk", attended_grad, values, preferred_element_type=jnp.float32
    )
    inner_sum = jnp.sum(prob_full * prob_grad, axis=-1, keepdims=True)
    score_grad = (prob_full * (prob_grad - inner_sum) * HEAD_SIZE ** (-0.5)).astype(jnp.bfloat16)
    query_grad = jnp.einsum(
        "sgrqk,skgd->sqgrd", score_grad, key_heads, preferred_element_type=jnp.float32
    )
    key_grad = jnp.einsum(
        "sgrqk,sqgrd->skgd", score_grad, queries, preferred_element_type=jnp.float32
    )
    value_grad = jnp.einsum(
        "sgrqk,sqgrd->skgd",
        prob_full.astype(jnp.bfloat16),
        attended_grad,
        preferred_element_type=jnp.float32,
    )
    projected_grad = jnp.concatenate(
        [
            unrotate(query_grad, cos_query, sin_query),
            unrotate(key_grad, cos_key, sin_key)[:, :, :, None],
            value_grad[:, :, :, None],
        ],
        axis=3,
    )
    projected_grad = projected_grad.astype(jnp.bfloat16).reshape(
        seq_count * length, groups * (repeat_factor + 2) * HEAD_SIZE
    )
    qkv_part = jnp.einsum("td,tc->dc", normed1, projected_grad, preferred_element_type=jnp.float32)
    normed1_grad = narrow(
        jnp.einsum("tc,dc->td", projected_grad, qkv_full, preferred_element_type=jnp.float32)
    )
    attn_gain_part = jnp.sum(normed1_grad * residual * scale_attn, axis=0)
    input_grad = (hidden1_grad + norm_back(residual, scale_attn, gain_attn, normed1_grad)).astype(
        jnp.bfloat16
    )
    attn_gain_total, mlp_gain_total = lax.psum((attn_gain_part, mlp_gain_part), "tensor")
    attn_gain_grad, qkv_grad, gate_grad, up_grad, mlp_gain_grad = (
        lax.psum_scatter(
            attn_gain_total.astype(jnp.bfloat16), "dp", scatter_dimension=0, tiled=True
        ).astype(jnp.float32),
        lax.psum_scatter(
            qkv_part.astype(jnp.bfloat16), "dp", scatter_dimension=0, tiled=True
        ).astype(jnp.float32),
        lax.psum_scatter(
            gate_part.astype(jnp.bfloat16), "dp", scatter_dimension=0, tiled=True
        ).astype(jnp.float32),
        lax.psum_scatter(
            up_part.astype(jnp.bfloat16), "dp", scatter_dimension=0, tiled=True
        ).astype(jnp.float32),
        lax.psum_scatter(
            mlp_gain_total.astype(jnp.bfloat16), "dp", scatter_dimension=0, tiled=True
        ).astype(jnp.float32),
    )
    out_grad, down_grad = (
        lax.psum_scatter(
            out_part.astype(jnp.bfloat16), "dp", scatter_dimension=1, tiled=True
        ).astype(jnp.float32),
        lax.psum_scatter(
            down_part.astype(jnp.bfloat16), "dp", scatter_dimension=1, tiled=True
        ).astype(jnp.float32),
    )
    return (
        block_out,
        input_grad,
        attn_gain_grad,
        qkv_grad,
        out_grad,
        mlp_gain_grad,
        gate_grad,
        up_grad,
        down_grad,
    )


def solution(mesh):
    in_specs = (
        P(("dp", "tensor"), None),
        P(("dp", "tensor"), None),
        P("dp", None),
        P("dp"),
        P("dp", "tensor"),
        P("tensor", "dp"),
        P("dp"),
        P("dp", "tensor"),
        P("dp", "tensor"),
        P("tensor", "dp"),
    )
    out_specs = (
        P(("dp", "tensor"), None),
        P(("dp", "tensor"), None),
        P("dp"),
        P("dp", "tensor"),
        P("tensor", "dp"),
        P("dp"),
        P("dp", "tensor"),
        P("dp", "tensor"),
        P("tensor", "dp"),
    )
    return jax.shard_map(local, mesh=mesh, in_specs=in_specs, out_specs=out_specs, check_vma=False)
```

profile of v0, /device:TPU:0, one launch (start us, length us, event | category | flops | bytes accessed | tf_op | source)
XLA Modules:
  0.0 1224.5 jit_solution(13426383904669908466)
XLA Ops:
  11.7 15.8 %all-reduce.7 = (bf16[1536]{0:T(1024)(128)(2,1)S(1)}, bf16[1536]{0:T(1024)(128)(2,1)S(1)}) all-reduce(bf16[1536]{0:T(1024)(128)(2,1)S(1)} %dynamic-update-slice, bf16[1536]{0:T(1024)(128)(2,1)S(1)} %dynamic-update-slice.1), channel_id=1, replica_groups=mesh['dp'=8,'tensor'=4] {'dp'}, use_global_device_ids=true, to_apply=%add.1 | all-reduce | flops 3072 | bytes 12288
  41.7 91.6 %all-gather.10.cloned.1.call-done = bf16[1536,1536]{1,0:T(8,128)(2,1)} async-done(((bf16[384,1536]{1,0:T(8,128)(2,1)}), bf16[1536,1536]{1,0:T(8,128)(2,1)}) %all-gather.10.cloned.1.call-update) | async-done | bytes 4718608 | tf_op jit(solution)/shard_map/all_gather | solution.py:73
  133.3 9.2 fusion.62
  142.4 8.9 reshape.132
  155.8 5.6 slice.64
  161.4 5.5 slice.68
  166.9 11.5 fusion.58
  186.1 5.5 copy.64
  191.6 5.2 copy.65
  199.3 5.3 copy.66
  225.3 5.9 convolution_convert_fusion.2
  231.9 83.4 %reduce-scatter.10.cloned.1.call-done = bf16[384,1536]{1,0:T(8,128)(2,1)} async-done(((bf16[1536,1536]{1,0:T(8,128)(2,1)}), bf16[384,1536]{1,0:T(8,128)(2,1)}) %reduce-scatter.10.cloned.1.call-update) | async-done | bytes 1179664 | tf_op jit(solution)/shard_map/reduce_scatter | solution.py:132
  320.9 28.8 %all-gather.20.cloned.1.call-done = bf16[1536,1024]{1,0:T(8,128)(2,1)} async-done(((bf16[192,1024]{1,0:T(8,128)(2,1)}), bf16[1536,1024]{1,0:T(8,128)(2,1)}) %all-gather.20.cloned.1.call-update) | async-done | bytes 3145744 | tf_op jit(solution)/shard_map/all_gather | solution.py:97
  349.8 91.4 %all-gather.16.cloned.1.call-done = bf16[1536,1536]{1,0:T(8,128)(2,1)} async-done(((bf16[384,1536]{1,0:T(8,128)(2,1)}), bf16[1536,1536]{1,0:T(8,128)(2,1)}) %all-gather.16.cloned.1.call-update) | async-done | bytes 4718608 | tf_op jit(solution)/shard_map/all_gather | solution.py:73
  441.2 10.0 fusion.64
  451.2 22.5 %all-gather.18.cloned.1.call-done = bf16[1536,1024]{1,0:T(8,128)(2,1)} async-done(((bf16[192,1024]{1,0:T(8,128)(2,1)}), bf16[1536,1024]{1,0:T(8,128)(2,1)}) %all-gather.18.cloned.1.call-update) | async-done | bytes 3145744 | tf_op jit(solution)/shard_map/all_gather | solution.py:96
  473.7 9.7 fusion.63
  483.4 24.4 %all-gather.22.cloned.1.call-done = bf16[1024,1536]{0,1:T(8,128)(2,1)} async-done(((bf16[1024,192]{0,1:T(8,128)(2,1)}), bf16[1024,1536]{0,1:T(8,128)(2,1)}) %all-gather.22.cloned.1.call-update) | async-done | bytes 3145744 | tf_op jit(solution)/shard_map/all_gather | solution.py:103
  507.8 91.0 %all-gather.24.cloned.1.call-done = bf16[1536,1536]{1,0:T(8,128)(2,1)} async-done(((bf16[384,1536]{1,0:T(8,128)(2,1)}), bf16[1536,1536]{1,0:T(8,128)(2,1)}) %all-gather.24.cloned.1.call-update) | async-done | bytes 4718608 | tf_op jit(solution)/shard_map/all_gather | solution.py:73
  598.8 14.1 %multiply_convert_fusion = (bf16[1536,1024]{1,0:T(8,128)(2,1)S(1)}, bf16[1536,1024]{1,0:T(8,128)(2,1)S(1)}, bf16[1536,1024]{1,0:T(8,128)(2,1)}) fusion(f32[1536,1024]{1,0:T(8,128)} %fusion.63, f32[1536,1024]{1,0:T(8,128)} %fusion.64, bf16[1536,1536]{1,0:T(8,128)(2,1)} %all-gather.24.cloned.1.call-done, bf16[1024,1536]{0,1:T(8,128)(2,1)} %all-gather.22.cloned.1.call-done), kind=kOutput, calls=%fused_computation.15 | convolution fusion | flops 4857004032 | bytes 29884416 | tf_op jit(solution)/shard_map/td,fd->tf/dot_general | solution.py:149
  612.9 5.1 fusion.65
  618.1 7.6 add_convert_fusion
  625.8 83.8 %reduce-scatter.14.cloned.1.call-done = bf16[384,1536]{1,0:T(8,128)(2,1)} async-done(((bf16[1536,1536]{1,0:T(8,128)(2,1)}), bf16[384,1536]{1,0:T(8,128)(2,1)}) %reduce-scatter.14.cloned.1.call-update) | async-done | bytes 1179664 | tf_op jit(solution)/shard_map/reduce_scatter | solution.py:77
  715.0 9.3 convolution_convert_fusion.3
  724.4 9.8 convolution_convert_fusion.4
  734.2 9.4 convolution_convert_fusion.5
  743.7 61.3 %all-gather.26.cloned.1.call-done = bf16[1536,1536]{1,0:T(8,128)(2,1)} async-done(((bf16[384,1536]{1,0:T(8,128)(2,1)}), bf16[1536,1536]{1,0:T(8,128)(2,1)}) %all-gather.26.cloned.1.call-update) | async-done | bytes 4718608 | tf_op jit(solution)/shard_map/all_gather | solution.py:165
  805.0 6.0 convolution_convert_fusion.8
  811.0 6.0 reshape.136
  816.9 4.8 copy.50
  821.8 7.8 fusion.39
  829.6 21.1 %broadcast_multiply_fusion = (f32[3,512,2,96]{1,3,2,0:T(8,128)}, f32[3,512,2,96]{1,3,2,0:T(8,128)}) fusion(f32[3,512,96]{1,2,0:T(8,128)S(1)} %copy-done.12, bf16[3,512,2,2,96]{1,4,3,2,0:T(8,128)(2,1)} %copy-done.17, f32[3,2,512,512,2]{3,2,4,1,0:T(8,128)} %fusion.39, f32[3,2,512,512,2]{3,2,4,1,0:T(8,128)} %copy-done.1, f32[3,2,2,512]{3,2,1,0:T(2,128)} %copy-done.30, ...), kind=kOutput, calls=%fused_computation.89 | convolution fusion | flops 638884352 | bytes 30105600 | tf_op jit(solution)/shard_map/sgrqk,sqgrd->skgd/dot_general | solution.py:180
  853.1 25.2 %bitcast_multiply_fusion.1 = (f32[3,512,2,2,96]{1,4,3,2,0:T(8,128)}, f32[3,2,96,2,512]{4,2,3,1,0:T(8,128)}) fusion(f32[3,512,96]{1,2,0:T(8,128)S(1)} %copy-done.12, bf16[3,512,2,96,1]{1,3,4,2,0:T(8,128)(2,1)S(1)} %copy-done.21, f32[3,2,512,512,2]{3,2,4,1,0:T(8,128)} %fusion.39, f32[3,2,512,512,2]{3,2,4,1,0:T(8,128)} %copy-done.1, ...), kind=kOutput, calls=%fused_computation.59 | convolution fusion | flops 639179264 | bytes 31875072 | tf_op jit(solution)/shard_map/sgrqk,skgd->sqgrd/dot_general | solution.py:177
  881.9 6.2 convolution_convert_fusion.7
  893.2 6.8 fusion.33
  901.6 5.7 copy.55
  907.3 6.6 convert_element_type.166
  913.9 8.9 convolution_convert_fusion.6
  922.8 8.4 convolution_convert_fusion.1
  931.6 9.3 convolution_convert_fusion
  945.7 5.9 reduce-scatter.22.cloned.1.call-done
  953.5 37.9 %reduce-scatter.20.cloned.1.call-done = bf16[384,192]{0,1:T(8,128)(2,1)} async-done(((bf16[384,1536]{0,1:T(8,128)(2,1)}), bf16[384,192]{0,1:T(8,128)(2,1)}) %reduce-scatter.20.cloned.1.call-update) | async-done | bytes 147472 | tf_op jit(solution)/shard_map/reduce_scatter | solution.py:227
  993.0 43.9 %reduce-scatter.18.cloned.1.call-done = bf16[192,768]{1,0:T(8,128)(2,1)} async-done(((bf16[1536,768]{1,0:T(8,128)(2,1)}), bf16[192,768]{1,0:T(8,128)(2,1)}) %reduce-scatter.18.cloned.1.call-update) | async-done | bytes 294928 | tf_op jit(solution)/shard_map/reduce_scatter | solution.py:213
  1038.8 85.6 %reduce-scatter.16.cloned.1.call-done = bf16[384,1536]{1,0:T(8,128)(2,1)} async-done(((bf16[1536,1536]{1,0:T(8,128)(2,1)}), bf16[384,1536]{1,0:T(8,128)(2,1)}) %reduce-scatter.16.cloned.1.call-update) | async-done | bytes 1179664 | tf_op jit(solution)/shard_map/reduce_scatter | solution.py:77
  1127.0 19.9 %all-reduce.5 = (bf16[1536]{0:T(1024)(128)(2,1)}, bf16[1536]{0:T(1024)(128)(2,1)}) all-reduce(f32[1536]{0:T(1024)} %get-tuple-element.11, f32[1536]{0:T(1024)} %get-tuple-element.9), channel_id=1, replica_groups=mesh['dp'=8,'tensor'=4] {'tensor'}, use_global_device_ids=true, to_apply=%region_14.15 | all-reduce | flops 3072 | bytes 18432 | tf_op jit(solution)/shard_map/psum | solution.py:208
  1146.9 13.2 %all-reduce.6 = (bf16[1536]{0:T(1024)(128)(2,1)}, bf16[1536]{0:T(1024)(128)(2,1)}) all-reduce(bf16[1536]{0:T(1024)(128)(2,1)} %get-tuple-element.13, bf16[1536]{0:T(1024)(128)(2,1)} %get-tuple-element.14), channel_id=6, replica_groups=mesh['dp'=8,'tensor'=4] {'dp'}, use_global_device_ids=true, to_apply=%region_15.16.clone | all-reduce | flops 3072 | bytes 12288
  1164.0 48.7 %reduce-scatter.12.cloned.1.call-done = bf16[384,1536]{1,0:T(8,128)(2,1)} async-done(((bf16[1536,1536]{1,0:T(8,128)(2,1)}), bf16[384,1536]{1,0:T(8,128)(2,1)}) %reduce-scatter.12.cloned.1.call-update) | async-done | bytes 1179664 | tf_op jit(solution)/shard_map/reduce_scatter | solution.py:77
  1212.7 4.5 fusion.11
  (174 shorter events, 93.7 us)
Async XLA Ops:
  7.2 26.1 %copy-start.27 = (s32[3,512]{1,0:T(4,128)S(1)}, s32[3,512]{1,0:T(4,128)}, u32[]{:S(2)}) copy-start(s32[3,512]{1,0:T(4,128)} %param.12) | copy-start | bytes 18436
  7.2 34.5 %all-gather.12.cloned.1.call-start = ((), (), s32[]{:S(2)}) async-start(), calls=%async_computation.10 | async-start | bytes 2654208 | tf_op jit(solution)/shard_map/all_gather | solution.py:95
  7.9 125.3 %all-gather.10.cloned.1.call-start = ((), (), s32[]{:S(2)}) async-start(), calls=%async_computation.9 | async-start | bytes 5898240 | tf_op jit(solution)/shard_map/all_gather | solution.py:73
  27.5 5.6 copy-start.25
  29.7 3.4 copy-start.29
  32.3 193.0 %all-gather.14.cloned.1.call-start = ((), (), s32[]{:S(2)}) async-start(), calls=%async_computation.11 | async-start | bytes 1327104 | tf_op jit(solution)/shard_map/all_gather | solution.py:102
  33.1 282.2 %reduce-scatter.10.cloned.1.call-start = ((), (), s32[]{:S(2)}) async-start(), calls=%async_computation.12 | async-start | bytes 5898240 | tf_op jit(solution)/shard_map/reduce_scatter | solution.py:132
  35.5 179.2 %copy-start.9 = (pred[3,512,512]{1,2,0:T(8,128)(4,1)}, pred[3,512,512]{1,2,0:T(8,128)(4,1)S(1)}, u32[]{:S(2)}) copy-start(pred[3,512,512]{1,2,0:T(8,128)(4,1)S(1)} %compare_and_fusion) | copy-start | bytes 2359300
  37.5 169.0 %copy-start.3 = (f32[3,512,96]{1,2,0:T(8,128)}, f32[3,512,96]{1,2,0:T(8,128)S(1)}, u32[]{:S(2)}) copy-start(f32[3,512,96]{1,2,0:T(8,128)S(1)} %get-tuple-element.46) | copy-start | bytes 1769476
  196.8 7.8 copy-start.11
  209.3 2.6 copy-start.17
  211.9 4.5 copy-start.1
  211.9 4.5 copy-start.18
  216.4 4.3 copy-start.30
  225.3 5.9 copy-start.23
  231.2 84.1 %copy-start = (bf16[384,1536]{1,0:T(8,128)(2,1)S(1)}, bf16[384,1536]{1,0:T(8,128)(2,1)}, u32[]{:S(2)}) copy-start(bf16[384,1536]{1,0:T(8,128)(2,1)} %param.10) | copy-start | bytes 3538948
  231.2 118.5 %all-gather.20.cloned.1.call-start = ((), (), s32[]{:S(2)}) async-start(), calls=%async_computation.15 | async-start | bytes 3538944 | tf_op jit(solution)/shard_map/all_gather | solution.py:97
  231.8 209.3 %all-gather.16.cloned.1.call-start = ((), (), s32[]{:S(2)}) async-start(), calls=%async_computation.13 | async-start | bytes 5898240 | tf_op jit(solution)/shard_map/all_gather | solution.py:73
  317.1 395.2 %copy-start.28 = (f32[384]{0:T(512)}, f32[384]{0:T(512)S(1)}, u32[]{:S(2)}) copy-start(f32[384]{0:T(512)S(1)} %get-tuple-element.37) | copy-start | bytes 4612
  317.1 395.2 %copy-start.32 = (f32[384]{0:T(512)}, f32[384]{0:T(512)S(1)}, u32[]{:S(2)}) copy-start(f32[384]{0:T(512)S(1)} %get-tuple-element.36) | copy-start | bytes 4612
  318.6 155.1 %all-gather.18.cloned.1.call-start = ((), (), s32[]{:S(2)}) async-start(), calls=%async_computation.14 | async-start | bytes 3538944 | tf_op jit(solution)/shard_map/all_gather | solution.py:96
  319.4 188.4 %all-gather.22.cloned.1.call-start = ((), (), s32[]{:S(2)}) async-start(), calls=%async_computation.16 | async-start | bytes 3538944 | tf_op jit(solution)/shard_map/all_gather | solution.py:103
  320.1 278.6 %all-gather.24.cloned.1.call-start = ((), (), s32[]{:S(2)}) async-start(), calls=%async_computation.18 | async-start | bytes 5898240 | tf_op jit(solution)/shard_map/all_gather | solution.py:73
  320.9 388.7 %reduce-scatter.14.cloned.1.call-start = ((), (), s32[]{:S(2)}) async-start(), calls=%async_computation.19 | async-start | bytes 5898240 | tf_op jit(solution)/shard_map/reduce_scatter | solution.py:77
  598.8 14.1 %copy-start.35 = (bf16[1536,1024]{1,0:T(8,128)(2,1)S(1)}, bf16[1536,1024]{1,0:T(8,128)(2,1)}, u32[]{:S(2)}) copy-start(bf16[1536,1024]{1,0:T(8,128)(2,1)} %all-gather.18.cloned.1.call-done) | copy-start | bytes 9437188
  612.9 5.2 copy-start.37
  612.9 5.2 copy-start.38
  612.9 5.2 copy-start.34
  625.7 87.3 %copy-start.5 = (bf16[384,1536]{1,0:T(8,128)(2,1)S(1)}, bf16[384,1536]{1,0:T(8,128)(2,1)}, u32[]{:S(2)}) copy-start(bf16[384,1536]{1,0:T(8,128)(2,1)} %param.11) | copy-start | bytes 3538948
  625.7 179.3 %all-gather.26.cloned.1.call-start = ((), (), s32[]{:S(2)}) async-start(), calls=%async_computation.20 | async-start | bytes 5898240 | tf_op jit(solution)/shard_map/all_gather | solution.py:165
  709.6 3.4 copy-start.7
  714.9 226.7 %reduce-scatter.26.cloned.1.call-start = ((), (), s32[]{:S(2)}) async-start(), calls=%async_computation.26 | async-start | bytes 3538944 | tf_op jit(solution)/shard_map/reduce_scatter | solution.py:230
  724.3 219.3 %reduce-scatter.24.cloned.1.call-start = ((), (), s32[]{:S(2)}) async-start(), calls=%async_computation.25 | async-start | bytes 3538944 | tf_op jit(solution)/shard_map/reduce_scatter | solution.py:219
  734.2 217.4 %reduce-scatter.22.cloned.1.call-start = ((), (), s32[]{:S(2)}) async-start(), calls=%async_computation.24 | async-start | bytes 3538944 | tf_op jit(solution)/shard_map/reduce_scatter | solution.py:216
  743.6 61.4 %copy-start.36 = (bf16[384,1536]{0,1:T(8,128)(2,1)S(1)}, bf16[384,1536]{0,1:T(8,128)(2,1)}, u32[]{:S(2)}) copy-start(bf16[384,1536]{0,1:T(8,128)(2,1)} %all-gather.14.cloned.1.call-done) | copy-start | bytes 3538948
  743.6 247.7 %reduce-scatter.20.cloned.1.call-start = ((), (), s32[]{:S(2)}) async-start(), calls=%async_computation.23 | async-start | bytes 1327104 | tf_op jit(solution)/shard_map/reduce_scatter | solution.py:227
  811.0 10.8 copy-start.19
  821.8 7.9 copy-start.12
  829.6 23.5 %copy-start.21 = (bf16[3,512,2,96,1]{1,3,4,2,0:T(8,128)(2,1)S(1)}, bf16[3,512,2,96,1]{1,3,4,2,0:T(8,128)(2,1)}, u32[]{:S(2)}) copy-start(bf16[3,512,2,96,1]{1,3,4,2,0:T(8,128)(2,1)} %copy-done.20) | copy-start | bytes 1769476
  878.3 3.6 copy-start.24
  881.9 6.5 copy-start.4
  881.9 6.5 copy-start.22
  888.1 148.8 %reduce-scatter.18.cloned.1.call-start = ((), (), s32[]{:S(2)}) async-start(), calls=%async_computation.22 | async-start | bytes 2654208 | tf_op jit(solution)/shard_map/reduce_scatter | solution.py:213
  890.6 2.5 copy-start.31
  922.8 201.6 %reduce-scatter.16.cloned.1.call-start = ((), (), s32[]{:S(2)}) async-start(), calls=%async_computation.21 | async-start | bytes 5898240 | tf_op jit(solution)/shard_map/reduce_scatter | solution.py:77
  931.3 281.4 %reduce-scatter.12.cloned.1.call-start = ((), (), s32[]{:S(2)}) async-start(), calls=%async_computation.17 | async-start | bytes 5898240 | tf_op jit(solution)/shard_map/reduce_scatter | solution.py:77
  940.9 183.5 %copy-start.26 = (f32[1536]{0:T(1024)S(1)}, f32[1536]{0:T(1024)}, u32[]{:S(2)}) copy-start(f32[1536]{0:T(1024)} %copy-done.25) | copy-start | bytes 18436
  943.6 269.1 %copy-start.6 = (bf16[384,1536]{1,0:T(8,128)(2,1)S(1)}, bf16[384,1536]{1,0:T(8,128)(2,1)}, u32[]{:S(2)}) copy-start(bf16[384,1536]{1,0:T(8,128)(2,1)} %param.11) | copy-start | bytes 3538948
  (9 other events, 18.3 us)
Sparse Core Ops, SparseCore 0:
  9.9 31.7 all-gather.11
  43.8 89.4 all-gather.9
  135.2 22.3 all-gather.13
  231.4 83.8 reduce-scatter.9
  317.0 32.6 all-gather.19
  351.8 89.3 all-gather.15
  443.1 30.5 all-gather.17
  475.6 32.1 all-gather.21
  509.4 89.3 all-gather.23
  625.8 83.6 reduce-scatter.13
  715.1 89.8 all-gather.25
  808.2 44.4 reduce-scatter.25
  856.1 46.0 reduce-scatter.23
  905.4 46.0 reduce-scatter.21
  954.6 36.6 reduce-scatter.19
  994.6 42.3 reduce-scatter.17
  1039.1 85.2 reduce-scatter.15
  1126.6 86.1 reduce-scatter.11
where the time goes:
time: 1230 us; the launch traced here: 1220 us
  waiting for transfers between devices  809 us (66%)
  matrix products  197 us (16%)
  local copies, waits for them, and re-layouts  92.6 us (8%)
  other arithmetic  60 us (5%)
  blocking collectives  48.9 us (4%)
  between operations  16.6 us (1%)
    all_gather x3, waiting for transfers between devices, widen(): return lax.all_gather(shard_rows, 'tensor', axis=0, tiled=True)  274 us
    reduce_scatter x3, waiting for transfers between devices, narrow(): lax.psum_scatter(partial_value.astype(jnp.bfloat16), 'tensor', scatter_di...  218 us
    reduce_scatter x1, waiting for transfers between devices, local(): lax.psum_scatter(jnp.dot(attn_flat, out_cols, preferred_element_type=jnp....  83.4 us
    all_gather x1, waiting for transfers between devices, local(): grad_full = lax.all_gather(hidden1_rounded, 'tensor', axis=0, tiled=True)  61.3 us
    reduce_scatter x1, waiting for transfers between devices, local(): lax.psum_scatter(qkv_part.astype(jnp.bfloat16), 'dp', scatter_dimension=0...  43.9 us
    reduce_scatter x1, waiting for transfers between devices, local(): lax.psum_scatter(out_part.astype(jnp.bfloat16), 'dp', scatter_dimension=1...  37.9 us
    unnamed x2, blocking collectives  29 us
    all_gather x1, waiting for transfers between devices, local(): lax.all_gather(up_weight, 'dp', axis=0, tiled=True)  28.8 us
  transfers between devices with their start and end apart: 18, of which 15 were waited for; matrix products, arithmetic and copies ran while one was open for 25% of the time, Pallas kernels for 0%

commit v1 on v0

--- a/solution.py
+++ b/solution.py
@@ -9,6 +9,17 @@
 EPS = 1e-05
 ROPE_BASE = 100000.0
 NEG_FILL = -1e30
+
+
+def gather_around(x, axis, dim):
+    ways = lax.axis_size(axis)
+    pieces = [x]
+    for far in range(1, ways):
+        pieces.append(
+            lax.ppermute(pieces[far - 1], axis, [(d, (d - 1) % ways) for d in range(ways)])
+        )
+    line = jnp.concatenate(pieces, axis=dim)
+    return jnp.roll(line, lax.axis_index(axis) * x.shape[dim], axis=dim)
 
 
 def doc_positions(segments):
@@ -70,7 +81,7 @@
 
 
 def widen(shard_rows):
-    return lax.all_gather(shard_rows, "tensor", axis=0, tiled=True)
+    return gather_around(shard_rows, "tensor", 0)
 
 
 def narrow(partial_value):

time: 1230 us -> 1160 us (0.943)
  waiting for transfers between devices: 809 us -> 654 us
  other arithmetic: 60 us -> 110 us
  starting transfers between devices: 1.19 us -> 35.9 us
    all_gather x3 -> x0, waiting for transfers between devices: 274 us -> none  [widen(): return lax.all_gather(shard_rows, 'tensor', axis=0, tiled=True)]
    ppermute x0 -> x9, waiting for transfers between devices: none -> 174 us  [gather_around(): lax.ppermute(pieces[far - 1], axis, [(d, (d - 1) % ways) for d in range(w...]
    concatenate x0 -> x3, other arithmetic: none -> 53.2 us  [the longest x2 52.2 us: gather_around(): return jnp.roll(line, lax.axis_index(axis) * x.shape[dim], axis=dim)]
    ppermute x0 -> x9, starting transfers between devices: none -> 34.7 us  [gather_around(): lax.ppermute(pieces[far - 1], axis, [(d, (d - 1) % ways) for d in range(w...]
    all_gather x1, waiting for transfers between devices: 28.8 us -> 0.02 us  [local(): lax.all_gather(up_weight, 'dp', axis=0, tiled=True)]
    all_gather x1, waiting for transfers between devices: 24.4 us -> 0.01 us  [local(): lax.all_gather(down_weight, 'dp', axis=1, tiled=True)]
    all_gather x1, waiting for transfers between devices: 22.5 us -> 0.01 us  [local(): lax.all_gather(gate_weight, 'dp', axis=0, tiled=True)]
    reduce_scatter x1, waiting for transfers between devices: 83.4 us -> 98.1 us  [local(): lax.psum_scatter(jnp.dot(attn_flat, out_cols, preferred_element_type=jnp....]
  transfers between devices with their start and end apart: 18 -> 24, of which waited for: 15 -> 16; matrix products, arithmetic and copies ran while one was open for 25% -> 31% of each run, Pallas kernels for 0% -> 0%
where the time goes in v1:
time: 1160 us
  waiting for transfers between devices  654 us (56%)
  matrix products  196 us (17%)
  other arithmetic  110 us (9%)
  local copies, waits for them, and re-layouts  94.5 us (8%)
  blocking collectives  48.9 us (4%)
  starting transfers between devices  35.9 us (3%)
  between operations  16 us (1%)
    reduce_scatter x3, waiting for transfers between devices, narrow(): lax.psum_scatter(partial_value.astype(jnp.bfloat16), 'tensor', scatter_di...  231 us
    ppermute x9, waiting for transfers between devices, gather_around(): lax.ppermute(pieces[far - 1], axis, [(d, (d - 1) % ways) for d in range(w...  174 us
    reduce_scatter x1, waiting for transfers between devices, local(): lax.psum_scatter(jnp.dot(attn_flat, out_cols, preferred_element_type=jnp....  98.1 us
    all_gather x1, waiting for transfers between devices, local(): grad_full = lax.all_gather(hidden1_rounded, 'tensor', axis=0, tiled=True)  61.1 us
    concatenate x2, other arithmetic, gather_around(): return jnp.roll(line, lax.axis_index(axis) * x.shape[dim], axis=dim)  52.2 us
    reduce_scatter x1, waiting for transfers between devices, local(): lax.psum_scatter(qkv_part.astype(jnp.bfloat16), 'dp', scatter_dimension=0...  44.1 us
    reduce_scatter x1, waiting for transfers between devices, local(): lax.psum_scatter(out_part.astype(jnp.bfloat16), 'dp', scatter_dimension=1...  37.9 us
    ppermute x9, starting transfers between devices, gather_around(): lax.ppermute(pieces[far - 1], axis, [(d, (d - 1) % ways) for d in range(w...  34.7 us
  transfers between devices with their start and end apart: 24, of which 16 were waited for; matrix products, arithmetic and copies ran while one was open for 31% of the time, Pallas kernels for 0%

profile of v1, /device:TPU:0, one launch (start us, length us, event | category | flops | bytes accessed | tf_op | source)
XLA Modules:
  0.0 1156.1 jit_solution(12875089565219772265)
XLA Ops:
  11.7 15.8 %all-reduce.7 = (bf16[1536]{0:T(1024)(128)(2,1)S(1)}, bf16[1536]{0:T(1024)(128)(2,1)S(1)}) all-reduce(bf16[1536]{0:T(1024)(128)(2,1)S(1)} %dynamic-update-slice, bf16[1536]{0:T(1024)(128)(2,1)S(1)} %dynamic-update-slice.1), channel_id=1, replica_groups=mesh['dp'=8,'tensor'=4] {'dp'}, use_global_device_ids=true, to_apply=%add.1 | all-reduce | flops 3072 | bytes 12288
  35.0 23.0 %collective-permute-done = bf16[384,1536]{1,0:T(8,128)(2,1)S(1)} collective-permute-done((bf16[384,1536]{1,0:T(8,128)(2,1)S(1)}, bf16[384,1536]{1,0:T(8,128)(2,1)S(1)}, u32[]{:S(2)}, u32[]{:S(2)}) %collective-permute-start) | collective-permute-done | bytes 1179680 | tf_op jit(solution)/shard_map/ppermute | solution.py:19
  64.0 20.4 %collective-permute-done.1 = bf16[384,1536]{1,0:T(8,128)(2,1)} collective-permute-done((bf16[384,1536]{1,0:T(8,128)(2,1)S(1)}, bf16[384,1536]{1,0:T(8,128)(2,1)}, u32[]{:S(2)}, u32[]{:S(2)}) %collective-permute-start.1) | collective-permute-done | bytes 1179680 | tf_op jit(solution)/shard_map/ppermute | solution.py:19
  91.7 18.7 %collective-permute-done.2 = bf16[384,1536]{1,0:T(8,128)(2,1)S(1)} collective-permute-done((bf16[384,1536]{1,0:T(8,128)(2,1)}, bf16[384,1536]{1,0:T(8,128)(2,1)S(1)}, u32[]{:S(2)}, u32[]{:S(2)}) %collective-permute-start.2) | collective-permute-done | bytes 1179680 | tf_op jit(solution)/shard_map/ppermute | solution.py:19
  110.4 24.9 %fusion.23 = bf16[1536,1536]{1,0:T(8,128)(2,1)} fusion(s32[]{:T(128)S(6)} %select_n.26, bf16[384,1536]{1,0:T(8,128)(2,1)S(1)} %fusion.40, bf16[384,1536]{1,0:T(8,128)(2,1)} %copy-done.24, bf16[384,1536]{1,0:T(8,128)(2,1)} %collective-permute-done.1, bf16[384,1536]{1,0:T(8,128)(2,1)S(1)} %collective-permute-done.2), kind=kLoop, calls=%fused_computation.66 | loop fusion | flops 37748736 | bytes 9437188 | tf_op jit(solution)/shard_map/jit(_roll_dynamic)/concatenate | solution.py:22
  135.3 9.2 fusion.83
  144.5 8.9 reshape.132
  157.8 5.5 slice.64
  163.4 5.5 slice.68
  168.9 11.5 fusion.79
  188.1 5.5 copy.64
  201.3 5.3 copy.66
  228.3 5.5 convolution_convert_fusion.2
  239.3 98.1 %reduce-scatter.10.cloned.1.call-done = bf16[384,1536]{1,0:T(8,128)(2,1)} async-done(((bf16[1536,1536]{1,0:T(8,128)(2,1)}), bf16[384,1536]{1,0:T(8,128)(2,1)}) %reduce-scatter.10.cloned.1.call-update) | async-done | bytes 1179664 | tf_op jit(solution)/shard_map/reduce_scatter | solution.py:143
  345.0 25.4 %collective-permute-done.3 = bf16[384,1536]{1,0:T(8,128)(2,1)S(1)} collective-permute-done((bf16[384,1536]{1,0:T(8,128)(2,1)S(1)}, bf16[384,1536]{1,0:T(8,128)(2,1)S(1)}, u32[]{:S(2)}, u32[]{:S(2)}) %collective-permute-start.3) | collective-permute-done | bytes 1179680 | tf_op jit(solution)/shard_map/ppermute | solution.py:19
  375.7 20.1 %collective-permute-done.7 = bf16[384,1536]{1,0:T(8,128)(2,1)} collective-permute-done((bf16[384,1536]{1,0:T(8,128)(2,1)}, bf16[384,1536]{1,0:T(8,128)(2,1)}, u32[]{:S(2)}, u32[]{:S(2)}) %collective-permute-start.7) | collective-permute-done | bytes 1179680 | tf_op jit(solution)/shard_map/ppermute | solution.py:19
  400.1 20.9 %collective-permute-done.4 = bf16[384,1536]{1,0:T(8,128)(2,1)} collective-permute-done((bf16[384,1536]{1,0:T(8,128)(2,1)S(1)}, bf16[384,1536]{1,0:T(8,128)(2,1)}, u32[]{:S(2)}, u32[]{:S(2)}) %collective-permute-start.4) | collective-permute-done | bytes 1179680 | tf_op jit(solution)/shard_map/ppermute | solution.py:19
  425.5 20.9 %collective-permute-done.8 = bf16[384,1536]{1,0:T(8,128)(2,1)} collective-permute-done((bf16[384,1536]{1,0:T(8,128)(2,1)}, bf16[384,1536]{1,0:T(8,128)(2,1)}, u32[]{:S(2)}, u32[]{:S(2)}) %collective-permute-start.8) | collective-permute-done | bytes 1179680 | tf_op jit(solution)/shard_map/ppermute | solution.py:19
  446.4 24.4 %collective-permute-done.5 = bf16[384,1536]{1,0:T(8,128)(2,1)} collective-permute-done((bf16[384,1536]{1,0:T(8,128)(2,1)}, bf16[384,1536]{1,0:T(8,128)(2,1)}, u32[]{:S(2)}, u32[]{:S(2)}) %collective-permute-start.5) | collective-permute-done | bytes 1179680 | tf_op jit(solution)/shard_map/ppermute | solution.py:19
  470.8 27.3 %fusion.9 = (bf16[1536,1536]{1,0:T(8,128)(2,1)}, bf16[1536,1536]{1,0:T(8,128)(2,1)}) fusion(s32[]{:T(128)S(6)} %select_n.26, bf16[384,1536]{1,0:T(8,128)(2,1)S(1)} %copy-done.7, bf16[384,1536]{1,0:T(8,128)(2,1)} %collective-permute-done.6, bf16[384,1536]{1,0:T(8,128)(2,1)} %collective-permute-done.7, bf16[384,1536]{1,0:T(8,128)(2,1)} %collective-permute-done.8, ...), kind=kLoop, calls=%fused_computation.52 | loop fusion | flops 75497472 | bytes 18874372 | tf_op jit(solution)/shard_map/jit(_roll_dynamic)/concatenate | solution.py:22
  498.2 9.8 fusion.85
  508.0 9.8 fusion.84
  517.8 14.5 %multiply_convert_fusion = (bf16[1536,1024]{1,0:T(8,128)(2,1)S(1)}, bf16[1536,1024]{1,0:T(8,128)(2,1)S(1)}, bf16[1536,1024]{1,0:T(8,128)(2,1)}) fusion(f32[1536,1024]{1,0:T(8,128)} %fusion.84, f32[1536,1024]{1,0:T(8,128)} %fusion.85, bf16[1536,1536]{1,0:T(8,128)(2,1)} %get-tuple-element.47, bf16[1024,1536]{0,1:T(8,128)(2,1)} %all-gather.15.cloned.1.call-done), kind=kOutput, calls=%fused_computation.39 | convolution fusion | flops 4857004032 | bytes 29884416 | tf_op jit(solution)/shard_map/td,fd->tf/dot_general | solution.py:160
  537.5 7.2 add_convert_fusion
  544.8 96.6 %reduce-scatter.14.cloned.1.call-done = bf16[384,1536]{1,0:T(8,128)(2,1)} async-done(((bf16[1536,1536]{1,0:T(8,128)(2,1)}), bf16[384,1536]{1,0:T(8,128)(2,1)}) %reduce-scatter.14.cloned.1.call-update) | async-done | bytes 1179664 | tf_op jit(solution)/shard_map/reduce_scatter | solution.py:88
  646.8 9.5 convolution_convert_fusion.3
  656.4 9.7 convolution_convert_fusion.4
  666.2 9.4 convolution_convert_fusion.5
  675.7 61.1 %all-gather.17.cloned.1.call-done = bf16[1536,1536]{1,0:T(8,128)(2,1)} async-done(((bf16[384,1536]{1,0:T(8,128)(2,1)}), bf16[1536,1536]{1,0:T(8,128)(2,1)}) %all-gather.17.cloned.1.call-update) | async-done | bytes 4718608 | tf_op jit(solution)/shard_map/all_gather | solution.py:176
  736.8 6.0 convolution_convert_fusion.8
  742.8 5.9 reshape.136
  753.5 7.8 fusion.60
  761.4 21.0 %broadcast_multiply_fusion = (f32[3,512,2,96]{1,3,2,0:T(8,128)}, f32[3,512,2,96]{1,3,2,0:T(8,128)}) fusion(f32[3,512,96]{1,2,0:T(8,128)S(1)} %copy-done.12, bf16[3,512,2,2,96]{1,4,3,2,0:T(8,128)(2,1)} %copy-done.17, f32[3,2,512,512,2]{3,2,4,1,0:T(8,128)} %fusion.60, f32[3,2,512,512,2]{3,2,4,1,0:T(8,128)} %copy-done.1, f32[3,2,2,512]{3,2,1,0:T(2,128)} %copy-done.33, ...), kind=kOutput, calls=%fused_computation.134 | convolution fusion | flops 638884352 | bytes 30105600 | tf_op jit(solution)/shard_map/sgrqk,sqgrd->skgd/dot_general | solution.py:191
  784.8 25.1 %bitcast_multiply_fusion.1 = (f32[3,512,2,2,96]{1,4,3,2,0:T(8,128)}, f32[3,2,96,2,512]{4,2,3,1,0:T(8,128)}) fusion(f32[3,512,96]{1,2,0:T(8,128)S(1)} %copy-done.12, bf16[3,512,2,96,1]{1,3,4,2,0:T(8,128)(2,1)S(1)} %copy-done.22, f32[3,2,512,512,2]{3,2,4,1,0:T(8,128)} %fusion.60, f32[3,2,512,512,2]{3,2,4,1,0:T(8,128)} %copy-done.1, ...), kind=kOutput, calls=%fused_computation.104 | convolution fusion | flops 639179264 | bytes 31875072 | tf_op jit(solution)/shard_map/sgrqk,skgd->sqgrd/dot_general | solution.py:188
  813.5 6.2 convolution_convert_fusion.7
  824.9 6.8 fusion.54
  833.3 5.7 copy.55
  839.1 6.6 convert_element_type.166
  845.6 8.9 convolution_convert_fusion.6
  854.6 8.4 convolution_convert_fusion.1
  863.3 9.3 convolution_convert_fusion
  877.5 6.0 reduce-scatter.22.cloned.1.call-done
  885.5 37.9 %reduce-scatter.20.cloned.1.call-done = bf16[384,192]{0,1:T(8,128)(2,1)} async-done(((bf16[384,1536]{0,1:T(8,128)(2,1)}), bf16[384,192]{0,1:T(8,128)(2,1)}) %reduce-scatter.20.cloned.1.call-update) | async-done | bytes 147472 | tf_op jit(solution)/shard_map/reduce_scatter | solution.py:238
  925.0 44.1 %reduce-scatter.18.cloned.1.call-done = bf16[192,768]{1,0:T(8,128)(2,1)} async-done(((bf16[1536,768]{1,0:T(8,128)(2,1)}), bf16[192,768]{1,0:T(8,128)(2,1)}) %reduce-scatter.18.cloned.1.call-update) | async-done | bytes 294928 | tf_op jit(solution)/shard_map/reduce_scatter | solution.py:224
  970.9 85.7 %reduce-scatter.16.cloned.1.call-done = bf16[384,1536]{1,0:T(8,128)(2,1)} async-done(((bf16[1536,1536]{1,0:T(8,128)(2,1)}), bf16[384,1536]{1,0:T(8,128)(2,1)}) %reduce-scatter.16.cloned.1.call-update) | async-done | bytes 1179664 | tf_op jit(solution)/shard_map/reduce_scatter | solution.py:88
  1059.2 19.9 %all-reduce.5 = (bf16[1536]{0:T(1024)(128)(2,1)}, bf16[1536]{0:T(1024)(128)(2,1)}) all-reduce(f32[1536]{0:T(1024)} %get-tuple-element.12, f32[1536]{0:T(1024)} %get-tuple-element.10), channel_id=1, replica_groups=mesh['dp'=8,'tensor'=4] {'tensor'}, use_global_device_ids=true, to_apply=%region_14.16 | all-reduce | flops 3072 | bytes 18432 | tf_op jit(solution)/shard_map/psum | solution.py:219
  1079.1 13.2 %all-reduce.6 = (bf16[1536]{0:T(1024)(128)(2,1)}, bf16[1536]{0:T(1024)(128)(2,1)}) all-reduce(bf16[1536]{0:T(1024)(128)(2,1)} %get-tuple-element.14, bf16[1536]{0:T(1024)(128)(2,1)} %get-tuple-element.15), channel_id=6, replica_groups=mesh['dp'=8,'tensor'=4] {'dp'}, use_global_device_ids=true, to_apply=%region_15.17.clone | all-reduce | flops 3072 | bytes 12288
  1096.1 48.7 %reduce-scatter.12.cloned.1.call-done = bf16[384,1536]{1,0:T(8,128)(2,1)} async-done(((bf16[1536,1536]{1,0:T(8,128)(2,1)}), bf16[384,1536]{1,0:T(8,128)(2,1)}) %reduce-scatter.12.cloned.1.call-update) | async-done | bytes 1179664 | tf_op jit(solution)/shard_map/reduce_scatter | solution.py:88
  (192 shorter events, 141.9 us)
Async XLA Ops:
  7.2 55.2 %copy-start.30 = (s32[3,512]{1,0:T(4,128)S(1)}, s32[3,512]{1,0:T(4,128)}, u32[]{:S(2)}) copy-start(s32[3,512]{1,0:T(4,128)} %param.14) | copy-start | bytes 18436
  7.2 128.1 %all-gather.7.cloned.1.call-start = ((), (), s32[]{:S(2)}) async-start(), calls=%async_computation.9 | async-start | bytes 2654208 | tf_op jit(solution)/shard_map/all_gather | solution.py:106
  7.9 219.4 %all-gather.9.cloned.1.call-start = ((), (), s32[]{:S(2)}) async-start(), calls=%async_computation.10 | async-start | bytes 1327104 | tf_op jit(solution)/shard_map/all_gather | solution.py:113
  27.5 62.5 %copy-start.28 = (f32[1536]{0:T(1024)}, f32[1536]{0:T(1024)S(1)}, u32[]{:S(2)}) copy-start(f32[1536]{0:T(1024)S(1)} %convert_element_type.141) | copy-start | bytes 18436
  29.7 32.7 %copy-start.32 = (f32[384]{0:T(512)}, f32[384]{0:T(512)S(1)}, u32[]{:S(2)}) copy-start(f32[384]{0:T(512)S(1)} %get-tuple-element.36) | copy-start | bytes 4612
  31.3 26.7 %collective-permute-start = (bf16[384,1536]{1,0:T(8,128)(2,1)S(1)}, bf16[384,1536]{1,0:T(8,128)(2,1)S(1)}, u32[]{:S(2)}, u32[]{:S(2)}) collective-permute-start(bf16[384,1536]{1,0:T(8,128)(2,1)S(1)} %fusion.40), channel_id=1, source_target_pairs={{0,3},{1,0},{2,1},{3,2},{4,7},{5,4},{6,5},{7,6},{8,11},{9,8},{10,9... | collective-permute-start | bytes 3538952 | tf_op jit(solution)/shard_map/ppermute | solution.py:19
  58.0 32.1 %copy-start.24 = (bf16[384,1536]{1,0:T(8,128)(2,1)}, bf16[384,1536]{1,0:T(8,128)(2,1)S(1)}, u32[]{:S(2)}) copy-start(bf16[384,1536]{1,0:T(8,128)(2,1)S(1)} %collective-permute-done) | copy-start | bytes 3538948
  58.0 26.4 %collective-permute-start.1 = (bf16[384,1536]{1,0:T(8,128)(2,1)S(1)}, bf16[384,1536]{1,0:T(8,128)(2,1)}, u32[]{:S(2)}, u32[]{:S(2)}) collective-permute-start(bf16[384,1536]{1,0:T(8,128)(2,1)S(1)} %collective-permute-done), channel_id=1, source_target_pairs={{0,3},{1,0},{2,1},{3,2},{4,7},{5,4},{6,5},{7,6},{8,11},{9,8},{10,9... | collective-permute-start | bytes 3538952 | tf_op jit(solution)/shard_map/ppermute | solution.py:19
  62.3 275.2 %reduce-scatter.10.cloned.1.call-start = ((), (), s32[]{:S(2)}) async-start(), calls=%async_computation.11 | async-start | bytes 5898240 | tf_op jit(solution)/shard_map/reduce_scatter | solution.py:143
  84.4 26.0 %collective-permute-start.2 = (bf16[384,1536]{1,0:T(8,128)(2,1)}, bf16[384,1536]{1,0:T(8,128)(2,1)S(1)}, u32[]{:S(2)}, u32[]{:S(2)}) collective-permute-start(bf16[384,1536]{1,0:T(8,128)(2,1)} %collective-permute-done.1), channel_id=1, source_target_pairs={{0,3},{1,0},{2,1},{3,2},{4,7},{5,4},{6,5},{7,6},{8,11},{9,8},{10,9... | collective-permute-start | bytes 3538952 | tf_op jit(solution)/shard_map/ppermute | solution.py:19
  90.1 118.5 %copy-start.3 = (f32[3,512,96]{1,2,0:T(8,128)}, f32[3,512,96]{1,2,0:T(8,128)S(1)}, u32[]{:S(2)}) copy-start(f32[3,512,96]{1,2,0:T(8,128)S(1)} %pad_maximum_fusion.1) | copy-start | bytes 1769476
  91.7 125.0 %copy-start.9 = (pred[3,512,512]{1,2,0:T(8,128)(4,1)}, pred[3,512,512]{1,2,0:T(8,128)(4,1)S(1)}, u32[]{:S(2)}) copy-start(pred[3,512,512]{1,2,0:T(8,128)(4,1)S(1)} %compare_and_fusion) | copy-start | bytes 2359300
  198.9 7.8 copy-start.11
  213.9 4.5 copy-start.1
  213.9 4.5 copy-start.19
  233.8 103.6 %copy-start = (bf16[384,1536]{1,0:T(8,128)(2,1)S(1)}, bf16[384,1536]{1,0:T(8,128)(2,1)}, u32[]{:S(2)}) copy-start(bf16[384,1536]{1,0:T(8,128)(2,1)} %param.12) | copy-start | bytes 3538948
  233.9 264.3 %all-gather.13.cloned.1.call-start = ((), (), s32[]{:S(2)}) async-start(), calls=%async_computation.13 | async-start | bytes 3538944 | tf_op jit(solution)/shard_map/all_gather | solution.py:108
  234.4 273.6 %all-gather.11.cloned.1.call-start = ((), (), s32[]{:S(2)}) async-start(), calls=%async_computation.12 | async-start | bytes 3538944 | tf_op jit(solution)/shard_map/all_gather | solution.py:107
  235.0 282.7 %all-gather.15.cloned.1.call-start = ((), (), s32[]{:S(2)}) async-start(), calls=%async_computation.14 | async-start | bytes 3538944 | tf_op jit(solution)/shard_map/all_gather | solution.py:114
  235.1 109.0 %collective-permute-start.6 = (bf16[384,1536]{1,0:T(8,128)(2,1)S(1)}, bf16[384,1536]{1,0:T(8,128)(2,1)}, u32[]{:S(2)}, u32[]{:S(2)}) collective-permute-start(bf16[384,1536]{1,0:T(8,128)(2,1)S(1)} %copy-done.7), channel_id=1, source_target_pairs={{0,3},{1,0},{2,1},{3,2},{4,7},{5,4},{6,5},{7,6},{8,11},{9,8},{10,9... | collective-permute-start | bytes 3538952 | tf_op jit(solution)/shard_map/ppermute | solution.py:19
  339.3 304.9 %copy-start.31 = (f32[384]{0:T(512)}, f32[384]{0:T(512)S(1)}, u32[]{:S(2)}) copy-start(f32[384]{0:T(512)S(1)} %get-tuple-element.38) | copy-start | bytes 4612
  339.3 304.9 %copy-start.35 = (f32[384]{0:T(512)}, f32[384]{0:T(512)S(1)}, u32[]{:S(2)}) copy-start(f32[384]{0:T(512)S(1)} %get-tuple-element.37) | copy-start | bytes 4612
  339.8 30.7 %collective-permute-start.3 = (bf16[384,1536]{1,0:T(8,128)(2,1)S(1)}, bf16[384,1536]{1,0:T(8,128)(2,1)S(1)}, u32[]{:S(2)}, u32[]{:S(2)}) collective-permute-start(bf16[384,1536]{1,0:T(8,128)(2,1)S(1)} %multiply_convert_fusion.3), channel_id=1, source_target_pairs={{0,3},{1,0},{2,1},{3,2},{4,7},{5,4},{6,5},{7,6},{8,11},{9,8},{10,9... | collective-permute-start | bytes 3538952 | tf_op jit(solution)/shard_map/ppermute | solution.py:19
  344.1 51.7 %collective-permute-start.7 = (bf16[384,1536]{1,0:T(8,128)(2,1)}, bf16[384,1536]{1,0:T(8,128)(2,1)}, u32[]{:S(2)}, u32[]{:S(2)}) collective-permute-start(bf16[384,1536]{1,0:T(8,128)(2,1)} %collective-permute-done.6), channel_id=1, source_target_pairs={{0,3},{1,0},{2,1},{3,2},{4,7},{5,4},{6,5},{7,6},{8,11},{9,8},{10,9... | collective-permute-start | bytes 3538952 | tf_op jit(solution)/shard_map/ppermute | solution.py:19
  371.5 49.5 %collective-permute-start.4 = (bf16[384,1536]{1,0:T(8,128)(2,1)S(1)}, bf16[384,1536]{1,0:T(8,128)(2,1)}, u32[]{:S(2)}, u32[]{:S(2)}) collective-permute-start(bf16[384,1536]{1,0:T(8,128)(2,1)S(1)} %collective-permute-done.3), channel_id=1, source_target_pairs={{0,3},{1,0},{2,1},{3,2},{4,7},{5,4},{6,5},{7,6},{8,11},{9,8},{10,9... | collective-permute-start | bytes 3538952 | tf_op jit(solution)/shard_map/ppermute | solution.py:19
  395.8 50.6 %collective-permute-start.8 = (bf16[384,1536]{1,0:T(8,128)(2,1)}, bf16[384,1536]{1,0:T(8,128)(2,1)}, u32[]{:S(2)}, u32[]{:S(2)}) collective-permute-start(bf16[384,1536]{1,0:T(8,128)(2,1)} %collective-permute-done.7), channel_id=1, source_target_pairs={{0,3},{1,0},{2,1},{3,2},{4,7},{5,4},{6,5},{7,6},{8,11},{9,8},{10,9... | collective-permute-start | bytes 3538952 | tf_op jit(solution)/shard_map/ppermute | solution.py:19
  421.0 49.8 %collective-permute-start.5 = (bf16[384,1536]{1,0:T(8,128)(2,1)}, bf16[384,1536]{1,0:T(8,128)(2,1)}, u32[]{:S(2)}, u32[]{:S(2)}) collective-permute-start(bf16[384,1536]{1,0:T(8,128)(2,1)} %collective-permute-done.4), channel_id=1, source_target_pairs={{0,3},{1,0},{2,1},{3,2},{4,7},{5,4},{6,5},{7,6},{8,11},{9,8},{10,9... | collective-permute-start | bytes 3538952 | tf_op jit(solution)/shard_map/ppermute | solution.py:19
  425.4 216.0 %reduce-scatter.14.cloned.1.call-start = ((), (), s32[]{:S(2)}) async-start(), calls=%async_computation.16 | async-start | bytes 5898240 | tf_op jit(solution)/shard_map/reduce_scatter | solution.py:88
  517.8 14.6 %copy-start.38 = (bf16[1536,1024]{1,0:T(8,128)(2,1)S(1)}, bf16[1536,1024]{1,0:T(8,128)(2,1)}, u32[]{:S(2)}) copy-start(bf16[1536,1024]{1,0:T(8,128)(2,1)} %all-gather.11.cloned.1.call-done) | copy-start | bytes 9437188
  532.3 5.2 copy-start.40
  532.3 5.2 copy-start.41
  532.3 5.2 copy-start.37
  544.7 192.1 %all-gather.17.cloned.1.call-start = ((), (), s32[]{:S(2)}) async-start(), calls=%async_computation.17 | async-start | bytes 5898240 | tf_op jit(solution)/shard_map/all_gather | solution.py:176
  646.8 226.6 %reduce-scatter.26.cloned.1.call-start = ((), (), s32[]{:S(2)}) async-start(), calls=%async_computation.23 | async-start | bytes 3538944 | tf_op jit(solution)/shard_map/reduce_scatter | solution.py:241
  656.3 218.9 %reduce-scatter.24.cloned.1.call-start = ((), (), s32[]{:S(2)}) async-start(), calls=%async_computation.22 | async-start | bytes 3538944 | tf_op jit(solution)/shard_map/reduce_scatter | solution.py:230
  666.2 217.3 %reduce-scatter.22.cloned.1.call-start = ((), (), s32[]{:S(2)}) async-start(), calls=%async_computation.21 | async-start | bytes 3538944 | tf_op jit(solution)/shard_map/reduce_scatter | solution.py:227
  675.6 61.2 %copy-start.39 = (bf16[384,1536]{0,1:T(8,128)(2,1)S(1)}, bf16[384,1536]{0,1:T(8,128)(2,1)}, u32[]{:S(2)}) copy-start(bf16[384,1536]{0,1:T(8,128)(2,1)} %all-gather.9.cloned.1.call-done) | copy-start | bytes 3538948
  675.6 247.7 %reduce-scatter.20.cloned.1.call-start = ((), (), s32[]{:S(2)}) async-start(), calls=%async_computation.20 | async-start | bytes 1327104 | tf_op jit(solution)/shard_map/reduce_scatter | solution.py:238
  742.8 10.8 copy-start.20
  753.5 7.9 copy-start.12
  761.4 23.4 %copy-start.22 = (bf16[3,512,2,96,1]{1,3,4,2,0:T(8,128)(2,1)S(1)}, bf16[3,512,2,96,1]{1,3,4,2,0:T(8,128)(2,1)}, u32[]{:S(2)}) copy-start(bf16[3,512,2,96,1]{1,3,4,2,0:T(8,128)(2,1)} %copy-done.21) | copy-start | bytes 1769476
  813.5 6.7 copy-start.4
  813.5 6.7 copy-start.23
  819.7 149.3 %reduce-scatter.18.cloned.1.call-start = ((), (), s32[]{:S(2)}) async-start(), calls=%async_computation.19 | async-start | bytes 2654208 | tf_op jit(solution)/shard_map/reduce_scatter | solution.py:224
  854.6 202.0 %reduce-scatter.16.cloned.1.call-start = ((), (), s32[]{:S(2)}) async-start(), calls=%async_computation.18 | async-start | bytes 5898240 | tf_op jit(solution)/shard_map/reduce_scatter | solution.py:88
  863.1 281.8 %reduce-scatter.12.cloned.1.call-start = ((), (), s32[]{:S(2)}) async-start(), calls=%async_computation.15 | async-start | bytes 5898240 | tf_op jit(solution)/shard_map/reduce_scatter | solution.py:88
  872.6 183.9 %copy-start.29 = (f32[1536]{0:T(1024)S(1)}, f32[1536]{0:T(1024)}, u32[]{:S(2)}) copy-start(f32[1536]{0:T(1024)} %copy-done.28) | copy-start | bytes 18436
  875.3 269.6 %copy-start.6 = (bf16[384,1536]{1,0:T(8,128)(2,1)S(1)}, bf16[384,1536]{1,0:T(8,128)(2,1)}, u32[]{:S(2)}) copy-start(bf16[384,1536]{1,0:T(8,128)(2,1)} %reduce-scatter.14.cloned.1.call-done) | copy-start | bytes 3538948
  (18 other events, 42.3 us)
Sparse Core Ops, SparseCore 0:
  9.9 31.7 all-gather.6
  62.4 21.4 all-gather.8
  234.0 103.4 reduce-scatter.9
  339.2 43.4 all-gather.12
  384.4 32.1 all-gather.10
  425.5 39.7 all-gather.14
  544.9 96.4 reduce-scatter.13
  646.9 89.8 all-gather.16
  740.2 44.4 reduce-scatter.25
  787.9 46.0 reduce-scatter.23
  837.4 46.0 reduce-scatter.21
  886.6 36.6 reduce-scatter.19
  926.7 42.3 reduce-scatter.17
  971.2 85.2 reduce-scatter.15
  1058.7 86.1 reduce-scatter.11
